TPU v7x, 32 devices: a whole 2x2x4 slice. The times are simulated.
32 devices in a mesh: freq: 8 (over z, core), tm: 4 (over y, x).
Axes of the slice: x: 2, y: 2, z: 4, core: 2. Of those that a mesh axis runs over, the one named last changes fastest.
Arguments:
- band_state: float32 [2048, 4096], P('freq', 'tm'), may hold values from -2.5 to 2.5
- lower_rows: int32 [3, 2048], replicated, may hold values from 0 to 2047, as said below
- upper_rows: int32 [3, 2048], replicated, may hold values from 0 to 2047, as said below
- delays: int32 [3, 2048], replicated, may hold values from 0 to 1024, as said below
- counts: int32 [7], replicated, may hold values from 256 to 2048, as said below
Outputs:
- dedispersed: float32 [2048, 4096], P('freq', 'tm')
Inputs may be any that keep to these rules, and one draw needn't show every extreme that they name: `counts`: entry 8 - 8 / 2^k + b is the live row count of output sub-band b of iteration k; it lies between half and all of that sub-band's 2 * 2048 / 2^(3 - k) padded rows, and in every iteration some sub-band has all its rows live. With w = 2048 / 2^(3 - k), lower_rows[k, i] is a row of input sub-band 2 * floor(i / (2 * w)) whose position in that sub-band is below its live count (all w rows are live in iteration 0). With w = 2048 / 2^(3 - k), upper_rows[k, i] is a row of input sub-band 2 * floor(i / (2 * w)) + 1 whose position in that sub-band is below its live count (all w rows are live in iteration 0). delays[k, i] is at most 2048 / 2^(3 - k), and equals it at some row in every iteration.
All inputs are finite; a program needn't handle non-finite values.
Results may differ from a plain program's by a relative error of at most 0.0003.
Values sent between devices are 32-bit elements; how exact they have to be, the bound alone decides.
No kernel may reach another device: no remote copies, remote signals or barrier semaphores. Data moves between devices by JAX's collectives and lax.ppermute only.
A program may use at most 64 MiB of HBM per device.

v0:
```python
import jax
import jax.numpy as jnp
from jax import lax
from jax.sharding import PartitionSpec as P

DMAX = 2048
ITERS = 3


def shifted_2(block, axis, distance):
    devices = range(lax.axis_size(axis))
    route = [(i - distance, i) for i in devices if i - distance in devices]
    return lax.ppermute(block, axis, route)


def delay_columns(extended, shifts, widest):
    row_count = extended.shape[0]
    for bit_index in range(widest.bit_length()):
        stride = 1 << bit_index
        shifted = jnp.concatenate(
            [jnp.zeros((row_count, stride), extended.dtype), extended[:, :-stride]], axis=1
        )
        extended = jnp.where((shifts >> bit_index & 1)[:, None] == 1, shifted, extended)
    return extended


def live_mask(global_rows, counts, width_out, offset, bands_out):
    band_index = global_rows // width_out
    band_counts = counts[offset : offset + bands_out]
    matches = band_index[:, None] == jnp.arange(bands_out, dtype=jnp.int32)[None, :]
    live_count = jnp.sum(jnp.where(matches, band_counts[None, :], 0), axis=1)
    return global_rows % width_out < live_count


def per_device(band_state, lower_rows, upper_rows, delays, counts):
    row_count, samples = band_state.shape
    freq_index = lax.axis_index("freq")
    first_row = freq_index * row_count
    global_rows = first_row + jnp.arange(row_count, dtype=jnp.int32)
    current = band_state
    for iteration in range(ITERS):
        width_in = DMAX >> ITERS - iteration
        width_out = 2 * width_in
        bands_out = DMAX // width_out
        offset = 2**ITERS - 2 ** (ITERS - iteration)
        lower_source = lax.dynamic_slice_in_dim(lower_rows[iteration], first_row, row_count)
        upper_source = lax.dynamic_slice_in_dim(upper_rows[iteration], first_row, row_count)
        own_delays = lax.dynamic_slice_in_dim(delays[iteration], first_row, row_count)
        gathered = lax.all_gather(current, "freq", axis=0, tiled=True)
        lower_values = jnp.take(gathered, lower_source, axis=0)
        upper_values = jnp.take(gathered, upper_source, axis=0)
        rim_columns = shifted_2(upper_values[:, samples - width_in :], "tm", 1)
        extended = jnp.concatenate([rim_columns, upper_values], axis=1)
        delayed = delay_columns(extended, own_delays, width_in)[:, width_in:]
        live_rows = live_mask(global_rows, counts, width_out, offset, bands_out)
        current = jnp.where(live_rows[:, None], lower_values + delayed, jnp.zeros_like(delayed))
    return current


def solution(mesh):
    return jax.shard_map(
        per_device,
        mesh=mesh,
        in_specs=(P("freq", "tm"), P(), P(), P(), P()),
        out_specs=P("freq", "tm"),
        check_vma=False,
    )
```

profile of v0, /device:TPU:4, one launch (start us, length us, event | category | flops | bytes accessed | tf_op | source)
XLA Modules:
  0.0 349.1 jit_solution(9411557968534590565)
XLA Ops:
  6.5 0.7 all-gather.4.cloned.1.call-update
  7.3 0.9 fusion.17
  8.2 0.9 fusion.19
  9.2 0.7 select_reduce_fusion
  9.9 0.9 fusion.18
  10.8 81.4 %all-gather.4.cloned.1.call-done = f32[2048,1024]{1,0:T(8,128)} async-done(((f32[256,1024]{1,0:T(8,128)}), f32[2048,1024]{1,0:T(8,128)}) %all-gather.4.cloned.1.call-update) | async-done | bytes 8388624 | tf_op jit(solution)/shard_map/all_gather | solution.py:49
  92.2 4.9 %gather_fusion.1 = f32[256,1024]{1,0:T(8,128)S(1)} fusion(f32[2048,1024]{1,0:T(8,128)} %all-gather.4.cloned.1.call-done, s32[1024]{0:T(1024)S(1)} %pad_clamp_fusion.4), kind=kCustom, calls=%fused_computation.1.clone | custom fusion | bytes 2098176 | tf_op jit(solution)/shard_map/jit(_take)/gather | solution.py:51
  97.2 0.1 broadcast_select_fusion.2
  97.3 3.4 collective-permute-start
  100.8 4.9 %gather_fusion = f32[256,1024]{1,0:T(8,128)S(1)} fusion(f32[2048,1024]{1,0:T(8,128)} %all-gather.4.cloned.1.call-done, s32[1024]{0:T(1024)S(1)} %pad_clamp_fusion.5), kind=kCustom, calls=%fused_computation.clone | custom fusion | bytes 2098176 | tf_op jit(solution)/shard_map/jit(_take)/gather | solution.py:50
  105.8 2.8 collective-permute-done
  108.6 0.1 fusion.4
  108.7 0.5 fusion.5
  109.1 0.5 pad_select_fusion.23
  109.6 0.5 pad_select_fusion.22
  110.1 0.5 pad_select_fusion.21
  110.6 0.5 pad_select_fusion.20
  111.1 0.5 pad_select_fusion.19
  111.5 0.5 pad_select_fusion.18
  112.1 0.2 pad_select_fusion.17
  112.3 0.1 slice.210
  112.4 1.2 fusion.11
  114.1 79.4 %all-gather.6.cloned.1.call-done = f32[2048,1024]{1,0:T(8,128)} async-done(((f32[256,1024]{1,0:T(8,128)}), f32[2048,1024]{1,0:T(8,128)}) %all-gather.6.cloned.1.call-update) | async-done | bytes 8388624 | tf_op jit(solution)/shard_map/all_gather | solution.py:49
  193.5 4.9 %gather_fusion.3 = f32[256,1024]{1,0:T(8,128)S(1)} fusion(f32[2048,1024]{1,0:T(8,128)} %all-gather.6.cloned.1.call-done, s32[1024]{0:T(1024)S(1)} %pad_clamp_fusion.2), kind=kCustom, calls=%fused_computation.3.clone | custom fusion | bytes 2098176 | tf_op jit(solution)/shard_map/jit(_take)/gather | solution.py:51
  198.4 0.1 broadcast_select_fusion.1
  198.6 3.6 %collective-permute-start.1 = (f32[256,512]{1,0:T(8,128)S(1)}, f32[256,512]{1,0:T(8,128)S(1)}, u32[]{:S(2)}, u32[]{:S(2)}) collective-permute-start(f32[256,512]{1,0:T(8,128)S(1)} %slice.212), channel_id=1, source_target_pairs={{0,1},{1,2},{2,3},{4,5},{5,6},{6,7},{8,9},{9,10},{10,11},{12,13},{... | collective-permute-start | bytes 1572872 | tf_op jit(solution)/shard_map/ppermute | solution.py:13
  202.2 4.9 %gather_fusion.2 = f32[256,1024]{1,0:T(8,128)S(1)} fusion(f32[2048,1024]{1,0:T(8,128)} %all-gather.6.cloned.1.call-done, s32[1024]{0:T(1024)S(1)} %pad_clamp_fusion.3), kind=kCustom, calls=%fused_computation.2.clone | custom fusion | bytes 2098176 | tf_op jit(solution)/shard_map/jit(_take)/gather | solution.py:50
  207.2 8.3 %collective-permute-done.1 = f32[256,512]{1,0:T(8,128)S(1)} collective-permute-done((f32[256,512]{1,0:T(8,128)S(1)}, f32[256,512]{1,0:T(8,128)S(1)}, u32[]{:S(2)}, u32[]{:S(2)}) %collective-permute-start.1) | collective-permute-done | bytes 524320 | tf_op jit(solution)/shard_map/ppermute | solution.py:13
  215.5 0.1 fusion.2
  215.6 0.6 fusion.3
  216.2 0.6 pad_select_fusion.16
  216.7 0.6 pad_select_fusion.15
  217.3 0.6 pad_select_fusion.14
  217.9 0.6 pad_select_fusion.13
  218.5 0.6 pad_select_fusion.12
  219.1 0.6 pad_select_fusion.11
  219.6 0.1 slice.221
  219.7 0.2 pad_select_fusion.10
  220.0 0.1 slice.222
  220.1 0.2 pad_select_fusion.9
  220.4 1.2 fusion.9
  221.7 79.7 %all-gather.8.cloned.1.call-done = f32[2048,1024]{1,0:T(8,128)} async-done(((f32[256,1024]{1,0:T(8,128)}), f32[2048,1024]{1,0:T(8,128)}) %all-gather.8.cloned.1.call-update) | async-done | bytes 8388624 | tf_op jit(solution)/shard_map/all_gather | solution.py:49
  301.4 4.9 %gather_fusion.5 = f32[256,1024]{1,0:T(8,128)S(1)} fusion(f32[2048,1024]{1,0:T(8,128)} %all-gather.8.cloned.1.call-done, s32[1024]{0:T(1024)S(1)} %pad_clamp_fusion), kind=kCustom, calls=%fused_computation.5.clone | custom fusion | bytes 2098176 | tf_op jit(solution)/shard_map/jit(_take)/gather | solution.py:51
  306.4 0.1 broadcast_select_fusion
  306.5 3.6 %collective-permute-start.2 = (f32[256,1024]{1,0:T(8,128)S(1)}, f32[256,1024]{1,0:T(8,128)S(1)}, u32[]{:S(2)}, u32[]{:S(2)}) collective-permute-start(f32[256,1024]{1,0:T(8,128)S(1)} %broadcast_select_fusion), channel_id=1, source_target_pairs={{0,1},{1,2},{2,3},{4,5},{5,6},{6,7},{8,9},{9,10},{10,11},{12,13},{... | collective-permute-start | bytes 3145736 | tf_op jit(solution)/shard_map/ppermute | solution.py:13
  310.1 0.6 slice.141
  310.7 0.7 fusion.13
  311.5 4.9 %gather_fusion.4 = f32[256,1024]{1,0:T(8,128)S(1)} fusion(f32[2048,1024]{1,0:T(8,128)} %all-gather.8.cloned.1.call-done, s32[1024]{0:T(1024)S(1)} %pad_clamp_fusion.1), kind=kCustom, calls=%fused_computation.4.clone | custom fusion | bytes 2098176 | tf_op jit(solution)/shard_map/jit(_take)/gather | solution.py:50
  316.4 18.2 %collective-permute-done.2 = f32[256,1024]{1,0:T(8,128)S(1)} collective-permute-done((f32[256,1024]{1,0:T(8,128)S(1)}, f32[256,1024]{1,0:T(8,128)S(1)}, u32[]{:S(2)}, u32[]{:S(2)}) %collective-permute-start.2) | collective-permute-done | bytes 1048608 | tf_op jit(solution)/shard_map/ppermute | solution.py:13
  334.6 0.1 fusion
  334.7 0.7 fusion.1
  335.5 0.7 pad_select_fusion.8
  336.2 0.7 pad_select_fusion.7
  337.0 0.7 pad_select_fusion.6
  337.8 0.7 pad_select_fusion.5
  338.5 0.7 pad_select_fusion.4
  339.3 0.7 pad_select_fusion.3
  340.0 0.2 slice.233
  340.2 0.3 pad_select_fusion.2
  340.5 0.1 slice.234
  340.6 0.3 pad_select_fusion.1
  340.9 0.1 slice.235
  341.0 0.2 pad_select_fusion
  341.3 1.3 fusion.7
  (41 shorter events, 0.9 us)
Async XLA Ops:
  6.5 85.7 %all-gather.4.cloned.1.call-start = ((), (), s32[]{:S(2)}) async-start(), calls=%async_computation | async-start | bytes 9437184 | tf_op jit(solution)/shard_map/all_gather | solution.py:49
  7.3 186.2 %all-gather.6.cloned.1.call-start = ((), (), s32[]{:S(2)}) async-start(), calls=%async_computation.1 | async-start | bytes 9437184 | tf_op jit(solution)/shard_map/all_gather | solution.py:49
  97.3 11.2 %collective-permute-start = (f32[256,256]{1,0:T(8,128)S(1)}, f32[256,256]{1,0:T(8,128)S(1)}, u32[]{:S(2)}, u32[]{:S(2)}) collective-permute-start(f32[256,256]{1,0:T(8,128)S(1)} %slice.200), channel_id=1, source_target_pairs={{0,1},{1,2},{2,3},{4,5},{5,6},{6,7},{8,9},{9,10},{10,11},{12,13},{... | collective-permute-start | bytes 786440 | tf_op jit(solution)/shard_map/ppermute | solution.py:13
  112.4 1.3 copy-start
  113.7 187.7 %all-gather.8.cloned.1.call-start = ((), (), s32[]{:S(2)}) async-start(), calls=%async_computation.2 | async-start | bytes 9437184 | tf_op jit(solution)/shard_map/all_gather | solution.py:49
  198.6 16.9 %collective-permute-start.1 = (f32[256,512]{1,0:T(8,128)S(1)}, f32[256,512]{1,0:T(8,128)S(1)}, u32[]{:S(2)}, u32[]{:S(2)}) collective-permute-start(f32[256,512]{1,0:T(8,128)S(1)} %slice.212), channel_id=1, source_target_pairs={{0,1},{1,2},{2,3},{4,5},{5,6},{6,7},{8,9},{9,10},{10,11},{12,13},{... | collective-permute-start | bytes 1572872 | tf_op jit(solution)/shard_map/ppermute | solution.py:13
  306.5 28.1 %collective-permute-start.2 = (f32[256,1024]{1,0:T(8,128)S(1)}, f32[256,1024]{1,0:T(8,128)S(1)}, u32[]{:S(2)}, u32[]{:S(2)}) collective-permute-start(f32[256,1024]{1,0:T(8,128)S(1)} %broadcast_select_fusion), channel_id=1, source_target_pairs={{0,1},{1,2},{2,3},{4,5},{5,6},{6,7},{8,9},{9,10},{10,11},{12,13},{... | collective-permute-start | bytes 3145736 | tf_op jit(solution)/shard_map/ppermute | solution.py:13
Sparse Core Ops, SparseCore 0:
  8.9 83.2 all-gather.3
  113.8 79.6 all-gather.5
  221.7 79.6 all-gather.7
where the time goes:
time: 350 us; the launch traced here: 349 us
  waiting for transfers between devices  271 us (77%)
  local copies, waits for them, and re-layouts  34.1 us (10%)
  other arithmetic  20.2 us (6%)
  between operations  13.7 us (4%)
  starting transfers between devices  10.6 us (3%)
    all_gather x3, waiting for transfers between devices, per_device(): gathered = lax.all_gather(current, 'freq', axis=0, tiled=True)  241 us
    ppermute x3, waiting for transfers between devices, shifted_2(): return lax.ppermute(block, axis, route)  29.3 us
    gather x3, local copies, waits for them, and re-layouts, per_device(): lower_values = jnp.take(gathered, lower_source, axis=0)  14.8 us
    gather x3, local copies, waits for them, and re-layouts, per_device(): upper_values = jnp.take(gathered, upper_source, axis=0)  14.8 us
    select_n x27, other arithmetic, delay_columns(): jnp.where((shifts >> bit_index & 1)[:, None] == 1, shifted, extended)  13.9 us
    ppermute x3, starting transfers between devices, shifted_2(): return lax.ppermute(block, axis, route)  10.5 us
  transfers between devices with their start and end apart: 6, of which 6 were waited for; matrix products, arithmetic and copies ran while one was open for 6% of the time, Pallas kernels for 0%

commit v1 on v0

--- a/solution.py
+++ b/solution.py
@@ -1,6 +1,10 @@
+from functools import partial
+
 import jax
 import jax.numpy as jnp
 from jax import lax
+from jax.experimental import pallas as pl
+from jax.experimental.pallas import tpu as pltpu
 from jax.sharding import PartitionSpec as P
 
 DMAX = 2048
@@ -56,10 +60,310 @@
         current = jnp.where(live_rows[:, None], lower_values + delayed, jnp.zeros_like(delayed))
     return current
 
+LANES = 128
+
+
+def as_index(value, multiple):
+    return pl.multiple_of(value, multiple)
+
+
+def linear_kernel(tail, block, lin, rim):
+    rows, samples = block.shape
+    pieces = samples // LANES
+
+    def step(group, carry):
+        for piece in range(pieces):
+            tile = block[pl.ds(as_index(group * 8, 8), 8), piece * LANES : (piece + 1) * LANES]
+            lin[pl.ds(group * 8 * pieces + piece, 8, stride=pieces), :] = tile
+            if piece >= pieces - tail:
+                rim[pl.ds(group * 8 * tail + piece - (pieces - tail), 8, stride=tail), :] = tile
+        return carry
+
+    lax.fori_loop(0, rows // 8, step, 0)
+
+
+def fill(stack, sources, slots, sems):
+    size = sources[0].shape[0]
+    copies = [
+        pltpu.make_async_copy(source, stack.at[pl.ds(as_index(slot * size, 8), size), :], sems.at[n])
+        for n, (source, slot) in enumerate(zip(sources, slots))
+    ]
+    for copy in copies:
+        copy.start()
+    return copies
+
+
+def live_limit(where, counts, iteration, rows):
+    spread = iteration + 1
+    offset = 2**ITERS - 2 ** (ITERS - iteration)
+    limit = counts[offset + lax.shift_right_logical(where, spread)]
+    return limit - (where & ((1 << spread) - 1)) * rows
+
+
+def delayed_sum(lower_of, delay_of, extended, pitch, reach, live_rows, row, lanes):
+    delay = delay_of(row)
+    whole = lax.shift_right_logical(delay, 7)
+    part = delay & (LANES - 1)
+    start = row * pitch + 8 + reach - whole
+    height = pitch - reach
+    near = extended[pl.ds(start, height), :]
+    past = extended[pl.ds(start - 1, height), :]
+    shifted = pltpu.roll(jnp.where(lanes < LANES - part, near, past), part, 1)
+    total = lower_of(row) + shifted
+    return jnp.where(row < live_rows, total, jnp.zeros_like(total))
+
+
+def first_kernel(rows, where, counts, lower_rows, upper_rows, delays, own, other, rim, merged, stack, extended, sems):
+    height = own.shape[0] // rows
+    reach = rim.shape[0] // rows
+    pitch = height + reach
+    me = where[0]
+    copies = fill(stack, (own, other), (me & 1, (me & 1) ^ 1), sems)
+    for copy in copies:
+        copy.wait()
+    base = me * rows
+    band = lax.shift_right_logical(me, 1) * (2 * rows)
+
+    def gather(row, carry):
+        source = upper_rows[0, base + row] - band
+        at = row * pitch + 8
+        extended[pl.ds(at, reach), :] = rim[pl.ds((source - rows) * reach, reach), :]
+        extended[pl.ds(at + reach, height), :] = stack[pl.ds(as_index(source * height, 8), height), :]
+        return carry
+
+    lax.fori_loop(0, rows, gather, 0, unroll=8)
+    lanes = lax.broadcasted_iota(jnp.int32, (height, LANES), 1)
+    live_rows = live_limit(me, counts, 0, rows)
+
+    def lower_of(row):
+        source = lower_rows[0, base + row] - band
+        return stack[pl.ds(as_index(source * height, 8), height), :]
+
+    def merge(row, carry):
+        merged[pl.ds(as_index(row * height, 8), height), :] = delayed_sum(
+            lower_of, lambda r: delays[0, base + r], extended, pitch, reach, live_rows, row, lanes
+        )
+        return carry
+
+    lax.fori_loop(0, rows, merge, 0, unroll=8)
+
+
+def pick_near_kernel(rows, iteration, where, lower_rows, upper_rows, a, b, c, d, low, high, rim, stack, sems):
+    height = a.shape[0] // rows
+    reach = rim.shape[0] // rows
+    me = where[0]
+    place = me & 3
+    copies = fill(stack, (a, b, c, d), (place, place ^ 1, place ^ 2, place ^ 3), sems)
+    for copy in copies:
+        copy.wait()
+    base = me * rows
+    band = lax.shift_right_logical(me, 2) * (4 * rows)
+
+    def step(row, carry):
+        source = lower_rows[iteration, base + row] - band
+        low[pl.ds(as_index(row * height, 8), height), :] = stack[pl.ds(as_index(source * height, 8), height), :]
+        source = upper_rows[iteration, base + row] - band
+        high[pl.ds(as_index(row * height, 8), height), :] = stack[pl.ds(as_index(source * height, 8), height), :]
+        rim[pl.ds(row * reach, reach), :] = stack[pl.ds(source * height + height - reach, reach), :]
+        return carry
+
+    lax.fori_loop(0, rows, step, 0, unroll=8)
+
+
+def pick_half_kernel(rows, iteration, far, where, lower_rows, upper_rows, a, b, c, d, *rest):
+    outs, (stack, sems) = rest[:-2], rest[-2:]
+    height = a.shape[0] // rows
+    me = where[0]
+    place = me & 3
+    slots = (place ^ 2, place ^ 3, place, place ^ 1) if far else (place, place ^ 1, place ^ 2, place ^ 3)
+    copies = fill(stack, (a, b, c, d), slots, sems)
+    for copy in copies:
+        copy.wait()
+    in_upper = lax.shift_right_logical(me, 2) ^ (1 if far else 0)
+    band = in_upper * (4 * rows)
+
+    def run(table):
+        def step(row, carry):
+            for out, base in zip(outs, (me * rows, (me ^ 2) * rows)):
+                source = table[iteration, base + row] - band
+                out[pl.ds(as_index(row * height, 8), height), :] = stack[
+                    pl.ds(as_index(source * height, 8), height), :
+                ]
+            return carry
+
+        lax.fori_loop(0, rows, step, 0, unroll=8)
+
+    @pl.when(in_upper == 0)
+    def _():
+        run(lower_rows)
+
+    @pl.when(in_upper == 1)
+    def _():
+        run(upper_rows)
+
+
+def join_kernel(rows, iteration, last, where, counts, delays, low, high, rim, merged, extended, *more):
+    height = low.shape[0] // rows
+    reach = rim.shape[0] // rows
+    pitch = height + reach
+    me = where[0]
+    base = me * rows
+
+    def gather(row, carry):
+        at = row * pitch + 8
+        extended[pl.ds(at, reach), :] = rim[pl.ds(row * reach, reach), :]
+        extended[pl.ds(at + reach, height), :] = high[pl.ds(as_index(row * height, 8), height), :]
+        return carry
+
+    lax.fori_loop(0, rows, gather, 0, unroll=8)
+    lanes = lax.broadcasted_iota(jnp.int32, (height, LANES), 1)
+    live_rows = live_limit(me, counts, iteration, rows)
+    target = more[0] if last else merged
+
+    def merge(row, carry):
+        target[pl.ds(as_index(row * height, 8), height), :] = delayed_sum(
+            lambda r: low[pl.ds(as_index(r * height, 8), height), :],
+            lambda r: delays[iteration, base + r], extended, pitch, reach, live_rows, row, lanes,
+        )
+        return carry
+
+    lax.fori_loop(0, rows, merge, 0, unroll=8)
+    if last:
+        def step(group, carry):
+            for piece in range(height):
+                merged[pl.ds(as_index(group * 8, 8), 8), piece * LANES : (piece + 1) * LANES] = target[
+                    pl.ds(group * 8 * height + piece, 8, stride=height), :
+                ]
+            return carry
+
+        lax.fori_loop(0, rows // 8, step, 0)
+
+
+SMEM = pl.BlockSpec(memory_space=pltpu.SMEM)
+VMEM = pl.BlockSpec(memory_space=pltpu.VMEM)
+HBM = pl.BlockSpec(memory_space=pl.ANY)
+
+
+def f32(*shape):
+    return jax.ShapeDtypeStruct(shape, jnp.float32)
+
+
+def scratch(*shape):
+    return pltpu.VMEM(shape, jnp.float32)
+
+
+def call(kernel, ins, outs, scratches, *args):
+    return pl.pallas_call(
+        kernel,
+        in_specs=list(ins),
+        out_specs=[VMEM] * len(outs),
+        out_shape=list(outs),
+        scratch_shapes=list(scratches),
+    )(*args)
+
+
+def hop(block, pairs):
+    return lax.ppermute(block, "freq", pairs)
+
+
+def merged_by_chips(band_state, lower_rows, upper_rows, delays, counts):
+    rows, samples = band_state.shape
+    height = samples // LANES
+    size = rows * height
+    devices = lax.axis_size("freq")
+    steps = lax.axis_size("tm")
+    where = lax.axis_index("freq").astype(jnp.int32)[None]
+    everyone = range(devices)
+
+    def twist(block, bits):
+        return hop(block, [(i, i ^ bits) for i in everyone])
+
+    def onward(block):
+        return lax.ppermute(block, "tm", [(t, t + 1) for t in range(steps - 1)])
+
+    reach = rows // LANES
+    lin, tail = call(
+        partial(linear_kernel, reach), [VMEM], [f32(size, LANES), f32(rows * reach, LANES)], [], band_state
+    )
+    other = twist(lin, 1)
+    grid = [(f, t) for f in everyone if f % 2 for t in range(steps - 1)]
+    straight = [(f * steps + t, f * steps + t + 1) for f, t in grid]
+    across = [(f * steps + t, (f - 1) * steps + t + 1) for f, t in grid]
+    rim_odd = lax.ppermute(tail, ("freq", "tm"), straight)
+    rim_even = lax.ppermute(tail, ("freq", "tm"), across)
+    rim = rim_odd + rim_even
+    (current,) = call(
+        partial(first_kernel, rows),
+        [SMEM] * 5 + [HBM] * 2 + [VMEM],
+        [f32(size, LANES)],
+        [scratch(2 * size, LANES), scratch(rows * (height + reach) + 16, LANES), pltpu.SemaphoreType.DMA((2,))],
+        where, counts, lower_rows, upper_rows, delays, lin, other, rim,
+    )
+
+    reach = 2 * reach
+    beside = twist(current, 1)
+    over = twist(current, 2)
+    diagonal = twist(over, 1)
+    stacked = [scratch(4 * size, LANES), pltpu.SemaphoreType.DMA((4,))]
+    low, high, rim = call(
+        partial(pick_near_kernel, rows, 1),
+        [SMEM] * 3 + [HBM] * 4,
+        [f32(size, LANES), f32(size, LANES), f32(rows * reach, LANES)],
+        stacked,
+        where, lower_rows, upper_rows, current, beside, over, diagonal,
+    )
+    (current,) = call(
+        partial(join_kernel, rows, 1, False),
+        [SMEM] * 3 + [VMEM] * 3,
+        [f32(size, LANES)],
+        [scratch(rows * (height + reach) + 16, LANES)],
+        where, counts, delays, low, high, onward(rim),
+    )
+
+    reach = 2 * reach
+    inner = hop(current, [(i, i ^ 6) for i in everyone if i & 2 != i >> 1 & 2])
+    outer = hop(current, [(i, i ^ 4) for i in everyone if i & 2 == i >> 1 & 2])
+    over = twist(current, 2)
+    beside = twist(current, 1)
+    inner_beside = twist(inner, 1)
+    outer_beside = twist(outer, 1)
+    diagonal = twist(over, 1)
+    (near,) = call(
+        partial(pick_half_kernel, rows, 2, False),
+        [SMEM] * 3 + [HBM] * 4, [f32(size, LANES)], stacked,
+        where, lower_rows, upper_rows, current, beside, over, diagonal,
+    )
+    far_own, far_next = call(
+        partial(pick_half_kernel, rows, 2, True),
+        [SMEM] * 3 + [HBM] * 4, [f32(size, LANES)] * 2, stacked,
+        where, lower_rows, upper_rows, inner, inner_beside, outer, outer_beside,
+    )
+    hub = where[0] & 2 != where[0] >> 1 & 2
+    handed = hop(far_next, [(i, i ^ 2) for i in everyone if i & 2 != i >> 1 & 2])
+    far = jnp.where(hub, far_own, handed)
+    in_upper = where[0] >> 2 == 1
+    low = jnp.where(in_upper, far, near)
+    high = jnp.where(in_upper, near, far)
+    (merged,) = call(
+        partial(join_kernel, rows, 2, True),
+        [SMEM] * 3 + [VMEM] * 3,
+        [f32(rows, samples)],
+        [scratch(rows * (height + reach) + 16, LANES), scratch(size, LANES)],
+        where, counts, delays, low, high, onward(high),
+    )
+    return merged
+
 
 def solution(mesh):
+    def body(band_state, *tables):
+        rows, samples = band_state.shape
+        fits = rows == DMAX >> ITERS and rows % LANES == 0 and samples == 8 * LANES
+        if ITERS == 3 and fits:
+            return merged_by_chips(band_state, *tables)
+        return per_device(band_state, *tables)
+
     return jax.shard_map(
-        per_device,
+        body,
         mesh=mesh,
         in_specs=(P("freq", "tm"), P(), P(), P(), P()),
         out_specs=P("freq", "tm"),

time: 350 us -> 207 us (0.59)
  waiting for transfers between devices: 271 us -> 139 us
  Pallas kernels: 0 us -> 43.3 us
  local copies, waits for them, and re-layouts: 34.1 us -> 4.81 us
  other arithmetic: 20.2 us -> 3.12 us
  between operations: 13.7 us -> 0.19 us
  starting transfers between devices: 10.6 us -> 15.7 us
    all_gather x3 -> x0, waiting for transfers between devices: 241 us -> none  [per_device(): gathered = lax.all_gather(current, 'freq', axis=0, tiled=True)]
    ppermute x3 -> x16, waiting for transfers between devices: 29.3 us -> 139 us  [the longest x12 88.5 us: hop(): return lax.ppermute(block, 'freq', pairs)]
    pallas_call x0 -> x7, Pallas kernels: none -> 43.3 us  [call(): pl.pallas_call(kernel, in_specs=list(ins), out_specs=[VMEM] * len(outs),...]
    gather x6 -> x0, local copies, waits for them, and re-layouts: 29.7 us -> none  [the longest x3 14.8 us: per_device(): lower_values = jnp.take(gathered, lower_source, axis=0)]
    select_n x40 -> x1, other arithmetic: 18.1 us -> 2.38 us  [merged_by_chips(): high = jnp.where(in_upper, near, far)]
    ppermute x3 -> x16, starting transfers between devices: 10.5 us -> 15.7 us  [the longest x12 9.93 us: hop(): return lax.ppermute(block, 'freq', pairs)]
    unnamed x2 -> x22, local copies, waits for them, and re-layouts: 0.01 us -> 4.81 us
    slice x16 -> x0, local copies, waits for them, and re-layouts: 4.36 us -> none  [the longest x9 0.96 us: delay_columns(): extended[:, :-stride]]
  transfers between devices with their start and end apart: 6 -> 16, of which waited for: 6 -> 8; matrix products, arithmetic and copies ran while one was open for 6% -> 0% of each run, Pallas kernels for 0% -> 6%
where the time goes in v1:
time: 207 us; the launch traced here: 206 us
  waiting for transfers between devices  139 us (67%)
  Pallas kernels  43.3 us (21%)
  starting transfers between devices  15.7 us (8%)
  local copies, waits for them, and re-layouts  4.81 us (2%)
  other arithmetic  3.12 us (2%)
    ppermute x12, waiting for transfers between devices, hop(): return lax.ppermute(block, 'freq', pairs)  88.5 us
    pallas_call x7, Pallas kernels, call(): pl.pallas_call(kernel, in_specs=list(ins), out_specs=[VMEM] * len(outs),...  43.3 us
    ppermute x2, waiting for transfers between devices, onward(): return lax.ppermute(block, 'tm', [(t, t + 1) for t in range(steps - 1)])  40.5 us
    ppermute x12, starting transfers between devices, hop(): return lax.ppermute(block, 'freq', pairs)  9.93 us
    ppermute x1, waiting for transfers between devices, merged_by_chips(): rim_even = lax.ppermute(tail, ('freq', 'tm'), across)  9.72 us
    unnamed x22, local copies, waits for them, and re-layouts  4.81 us
  transfers between devices with their start and end apart: 16, of which 8 were waited for; matrix products, arithmetic and copies ran while one was open for 0% of the time, Pallas kernels for 6%

profile of v1, /device:TPU:4, one launch (start us, length us, event | category | flops | bytes accessed | tf_op | source)
XLA Modules:
  0.0 205.9 jit_solution(4232261955806370375)
XLA Ops:
  0.0 2.6 %shard_map.55 = (f32[2048,128]{1,0:T(8,128)}, f32[512,128]{1,0:T(8,128)}) custom-call(f32[256,1024]{1,0:T(8,128)} %block.1), custom_call_target="tpu_custom_call" | custom-call | tf_op jit(solution)/shard_map/pallas_call | solution.py:256
  2.6 0.0 collective-permute-start
  2.6 0.7 collective-permute-start.1
  3.3 1.3 collective-permute-start.2
  4.6 0.0 collective-permute-done.1
  4.6 9.7 %collective-permute-done.2 = f32[512,128]{1,0:T(8,128)S(1)} collective-permute-done((f32[512,128]{1,0:T(8,128)}, f32[512,128]{1,0:T(8,128)S(1)}, u32[]{:S(2)}, u32[]{:S(2)}) %collective-permute-start.2) | collective-permute-done | bytes 262176 | tf_op jit(solution)/shard_map/ppermute | solution.py:293
  14.3 0.7 add.3.rim
  15.1 0.0 collective-permute-done.other
  15.1 0.0 copy-start.8
  15.1 1.0 copy-done.8
  16.0 8.9 %shard_map.56.a = f32[2048,128]{1,0:T(8,128)} custom-call(s32[1]{0:T(128)} %bitcast.where, s32[7]{0:T(128)} %counts.5, s32[3,2048]{1,0:T(4,128)} %lower_rows.7, s32[3,2048]{1,0:T(4,128)} %upper_rows.7, s32[3,2048]{1,0:T(4,128)} %delays.5, f32[2048,128]{1,0:T(8,128)} %get-tuple-element.12.own, f32[2048,128]{1,0:T(8,128)} %copy-done.8, f32[512,128]{1,0:T(8,128)} %add.3.rim), custom_call_target="tpu_custom_call" | custom-call | tf_op jit(solution)/shard_map/pallas_call | solution.py:256
  24.9 1.6 collective-permute-start.4
  26.5 0.0 collective-permute-start.3
  26.6 22.0 %collective-permute-done.4.c = f32[2048,128]{1,0:T(8,128)S(1)} collective-permute-done((f32[2048,128]{1,0:T(8,128)}, f32[2048,128]{1,0:T(8,128)S(1)}, u32[]{:S(2)}, u32[]{:S(2)}) %collective-permute-start.4) | collective-permute-done | bytes 1048608 | tf_op jit(solution)/shard_map/ppermute | solution.py:266
  48.6 0.0 copy-start.4
  48.6 0.0 collective-permute-start.5
  48.6 0.0 collective-permute-done.3.b
  48.6 0.0 copy-start.5
  48.6 2.6 %collective-permute-done.5.d = f32[2048,128]{1,0:T(8,128)S(1)} collective-permute-done((f32[2048,128]{1,0:T(8,128)S(1)}, f32[2048,128]{1,0:T(8,128)S(1)}, u32[]{:S(2)}, u32[]{:S(2)}) %collective-permute-start.5) | collective-permute-done | bytes 1048608 | tf_op jit(solution)/shard_map/ppermute | solution.py:266
  51.2 0.0 copy-done.4
  51.2 0.0 copy-done.5
  51.2 0.0 copy-start.6
  51.2 1.0 copy-done.6
  52.3 6.6 %shard_map.57 = (f32[2048,128]{1,0:T(8,128)}, f32[2048,128]{1,0:T(8,128)}, f32[1024,128]{1,0:T(8,128)}) custom-call(s32[1]{0:T(128)} %bitcast.where, s32[3,2048]{1,0:T(4,128)} %lower_rows.7, s32[3,2048]{1,0:T(4,128)} %upper_rows.7, f32[2048,128]{1,0:T(8,128)} %shard_map.56.a, f32[2048,128]{1,0:T(8,128)} %copy-done.5, f32[2048,128]{1,0:T(8,128)} %copy-done.4, ...), custom_call_target="tpu_custom_call" | custom-call | tf_op jit(solution)/shard_map/pallas_call | solution.py:256
  58.9 1.9 collective-permute-start.6
  60.8 15.0 %collective-permute-done.6.rim = f32[1024,128]{1,0:T(8,128)S(1)} collective-permute-done((f32[1024,128]{1,0:T(8,128)}, f32[1024,128]{1,0:T(8,128)S(1)}, u32[]{:S(2)}, u32[]{:S(2)}) %collective-permute-start.6) | collective-permute-done | bytes 524320 | tf_op jit(solution)/shard_map/ppermute | solution.py:282
  75.8 0.0 copy-start.10
  75.8 0.8 copy-done.10
  76.7 6.0 %shard_map.58.a = f32[2048,128]{1,0:T(8,128)} custom-call(s32[1]{0:T(128)} %bitcast.where, s32[7]{0:T(128)} %counts.5, s32[3,2048]{1,0:T(4,128)} %delays.5, f32[2048,128]{1,0:T(8,128)} %get-tuple-element.14.low, f32[2048,128]{1,0:T(8,128)} %get-tuple-element.15.high, f32[1024,128]{1,0:T(8,128)} %copy-done.10), custom_call_target="tpu_custom_call" | custom-call | tf_op jit(solution)/shard_map/pallas_call | solution.py:256
  82.7 4.5 %collective-permute-start.9 = (f32[2048,128]{1,0:T(8,128)}, f32[2048,128]{1,0:T(8,128)S(1)}, u32[]{:S(2)}, u32[]{:S(2)}) collective-permute-start(f32[2048,128]{1,0:T(8,128)} %shard_map.58.a), channel_id=1, source_target_pairs={{0,16},{4,20},{24,8},{28,12},{1,17},{5,21},{25,9},{29,13},{2,18},{... | collective-permute-start | bytes 3145736 | tf_op jit(solution)/shard_map/ppermute | solution.py:266
  87.2 0.7 collective-permute-start.7
  88.0 1.1 collective-permute-start.13
  89.1 22.0 %collective-permute-done.9.c = f32[2048,128]{1,0:T(8,128)S(1)} collective-permute-done((f32[2048,128]{1,0:T(8,128)}, f32[2048,128]{1,0:T(8,128)S(1)}, u32[]{:S(2)}, u32[]{:S(2)}) %collective-permute-start.9) | collective-permute-done | bytes 1048608 | tf_op jit(solution)/shard_map/ppermute | solution.py:266
  111.1 0.0 copy-start.1
  111.1 0.0 collective-permute-start.10
  111.1 0.0 collective-permute-done.7.a
  111.1 0.0 copy-start.2
  111.1 0.5 collective-permute-start.8
  111.6 0.1 collective-permute-start.12
  111.7 20.2 %collective-permute-done.13.c = f32[2048,128]{1,0:T(8,128)} collective-permute-done((f32[2048,128]{1,0:T(8,128)}, f32[2048,128]{1,0:T(8,128)}, u32[]{:S(2)}, u32[]{:S(2)}) %collective-permute-start.13) | collective-permute-done | bytes 1048608 | tf_op jit(solution)/shard_map/ppermute | solution.py:266
  131.9 0.0 collective-permute-start.14
  131.9 0.0 collective-permute-done.10.d
  131.9 0.0 copy-start.3
  131.9 0.0 collective-permute-done.8.b
  131.9 0.0 copy-done.1
  131.9 0.0 copy-done.2
  131.9 1.0 copy-done.3
  132.9 6.9 %shard_map.59 = (f32[2048,128]{1,0:T(8,128)}, f32[2048,128]{1,0:T(8,128)}) custom-call(s32[1]{0:T(128)} %bitcast.where, s32[3,2048]{1,0:T(4,128)} %lower_rows.7, s32[3,2048]{1,0:T(4,128)} %upper_rows.7, f32[2048,128]{1,0:T(8,128)} %copy-done.2, f32[2048,128]{1,0:T(8,128)} %collective-permute-done.8.b, f32[2048,128]{1,0:T(8,128)} %copy-done.1, ...), custom_call_target="tpu_custom_call" | custom-call | tf_op jit(solution)/shard_map/pallas_call | solution.py:256
  139.8 1.3 collective-permute-start.11
  141.1 0.0 copy-start.9
  141.1 0.0 collective-permute-done.12.b
  141.1 0.0 collective-permute-done.14.d
  141.1 5.9 %shard_map.60 = f32[2048,128]{1,0:T(8,128)} custom-call(s32[1]{0:T(128)} %bitcast.where, s32[3,2048]{1,0:T(4,128)} %lower_rows.7, s32[3,2048]{1,0:T(4,128)} %upper_rows.7, f32[2048,128]{1,0:T(8,128)} %shard_map.58.a, f32[2048,128]{1,0:T(8,128)} %collective-permute-done.12.b, f32[2048,128]{1,0:T(8,128)} %collective-permute-done.13.c, ...), custom_call_target="tpu_custom_call" | custom-call | tf_op jit(solution)/shard_map/pallas_call | solution.py:256
  147.1 21.6 %collective-permute-done.11 = f32[2048,128]{1,0:T(8,128)S(1)} collective-permute-done((f32[2048,128]{1,0:T(8,128)}, f32[2048,128]{1,0:T(8,128)S(1)}, u32[]{:S(2)}, u32[]{:S(2)}) %collective-permute-start.11) | collective-permute-done | bytes 1048608 | tf_op jit(solution)/shard_map/ppermute | solution.py:266
  168.7 0.0 copy-done.9
  168.7 2.4 %broadcast_select_fusion.1 = (f32[2048,128]{1,0:T(8,128)S(1)}, f32[2048,128]{1,0:T(8,128)}) fusion(f32[2048,128]{1,0:T(8,128)} %shard_map.60, pred[]{:T(512)S(6)} %eq.3, f32[2048,128]{1,0:T(8,128)S(1)} %copy-done.9, f32[2048,128]{1,0:T(8,128)S(1)} %collective-permute-done.11, pred[]{:T(512)S(6)} %ne.3), kind=kLoop, calls=%fused_computation.1 | loop fusion | flops 786432 | bytes 5242882 | tf_op jit(solution)/shard_map/jit(_where)/select_n | solution.py:346
  171.1 0.0 copy-start
  171.1 1.9 collective-permute-start.15
  173.0 25.5 %collective-permute-done.15.rim = f32[2048,128]{1,0:T(8,128)S(1)} collective-permute-done((f32[2048,128]{1,0:T(8,128)S(1)}, f32[2048,128]{1,0:T(8,128)S(1)}, u32[]{:S(2)}, u32[]{:S(2)}) %collective-permute-start.15) | collective-permute-done | bytes 1048608 | tf_op jit(solution)/shard_map/ppermute | solution.py:282
  198.5 0.0 copy-start.7
  198.5 0.0 copy-done
  198.5 1.0 copy-done.7
  199.5 6.4 %shard_map.61 = f32[256,1024]{1,0:T(8,128)} custom-call(s32[1]{0:T(128)} %bitcast.where, s32[7]{0:T(128)} %counts.5, s32[3,2048]{1,0:T(4,128)} %delays.5, f32[2048,128]{1,0:T(8,128)} %get-tuple-element.20.low, f32[2048,128]{1,0:T(8,128)} %copy-done, f32[2048,128]{1,0:T(8,128)} %copy-done.7), custom_call_target="tpu_custom_call" | custom-call | tf_op jit(solution)/shard_map/pallas_call | solution.py:256
Async XLA Ops:
  2.6 12.5 %collective-permute-start = (f32[2048,128]{1,0:T(8,128)}, f32[2048,128]{1,0:T(8,128)S(1)}, u32[]{:S(2)}, u32[]{:S(2)}) collective-permute-start(f32[2048,128]{1,0:T(8,128)} %get-tuple-element.12.own), channel_id=1, source_target_pairs={{0,4},{4,0},{8,12},{12,8},{16,20},{20,16},{24,28},{28,24},{1,5},{5... | collective-permute-start | bytes 3145736 | tf_op jit(solution)/shard_map/ppermute | solution.py:266
  2.6 2.0 collective-permute-start.1
  3.3 11.0 %collective-permute-start.2 = (f32[512,128]{1,0:T(8,128)}, f32[512,128]{1,0:T(8,128)S(1)}, u32[]{:S(2)}, u32[]{:S(2)}) collective-permute-start(f32[512,128]{1,0:T(8,128)} %get-tuple-element.13), channel_id=1, source_target_pairs={{4,1},{5,2},{6,3},{12,9},{13,10},{14,11},{20,17},{21,18},{22,19},{... | collective-permute-start | bytes 786440 | tf_op jit(solution)/shard_map/ppermute | solution.py:293
  15.1 1.0 copy-start.8
  24.9 23.7 %collective-permute-start.4 = (f32[2048,128]{1,0:T(8,128)}, f32[2048,128]{1,0:T(8,128)S(1)}, u32[]{:S(2)}, u32[]{:S(2)}) collective-permute-start(f32[2048,128]{1,0:T(8,128)} %shard_map.56.a), channel_id=1, source_target_pairs={{0,8},{4,12},{8,0},{12,4},{16,24},{20,28},{24,16},{28,20},{1,9},{5... | collective-permute-start | bytes 3145736 | tf_op jit(solution)/shard_map/ppermute | solution.py:266
  26.5 22.0 %collective-permute-start.3 = (f32[2048,128]{1,0:T(8,128)}, f32[2048,128]{1,0:T(8,128)S(1)}, u32[]{:S(2)}, u32[]{:S(2)}) collective-permute-start(f32[2048,128]{1,0:T(8,128)} %shard_map.56.a), channel_id=1, source_target_pairs={{0,4},{4,0},{8,12},{12,8},{16,20},{20,16},{24,28},{28,24},{1,5},{5... | collective-permute-start | bytes 3145736 | tf_op jit(solution)/shard_map/ppermute | solution.py:266
  48.6 2.7 %copy-start.4 = (f32[2048,128]{1,0:T(8,128)}, f32[2048,128]{1,0:T(8,128)S(1)}, u32[]{:S(2)}) copy-start(f32[2048,128]{1,0:T(8,128)S(1)} %collective-permute-done.4.c) | copy-start | bytes 3145732
  48.6 2.7 %collective-permute-start.5 = (f32[2048,128]{1,0:T(8,128)S(1)}, f32[2048,128]{1,0:T(8,128)S(1)}, u32[]{:S(2)}, u32[]{:S(2)}) collective-permute-start(f32[2048,128]{1,0:T(8,128)S(1)} %collective-permute-done.4.c), channel_id=1, source_target_pairs={{0,4},{4,0},{8,12},{12,8},{16,20},{20,16},{24,28},{28,24},{1,5},{5... | collective-permute-start | bytes 3145736 | tf_op jit(solution)/shard_map/ppermute | solution.py:266
  48.6 2.7 %copy-start.5 = (f32[2048,128]{1,0:T(8,128)}, f32[2048,128]{1,0:T(8,128)S(1)}, u32[]{:S(2)}) copy-start(f32[2048,128]{1,0:T(8,128)S(1)} %collective-permute-done.3.b) | copy-start | bytes 3145732
  51.2 1.0 copy-start.6
  58.9 17.0 %collective-permute-start.6 = (f32[1024,128]{1,0:T(8,128)}, f32[1024,128]{1,0:T(8,128)S(1)}, u32[]{:S(2)}, u32[]{:S(2)}) collective-permute-start(f32[1024,128]{1,0:T(8,128)} %get-tuple-element.16), channel_id=1, source_target_pairs={{0,1},{1,2},{2,3},{4,5},{5,6},{6,7},{8,9},{9,10},{10,11},{12,13},{... | collective-permute-start | bytes 1572872 | tf_op jit(solution)/shard_map/ppermute | solution.py:282
  75.8 0.8 copy-start.10
  82.7 28.4 %collective-permute-start.9 = (f32[2048,128]{1,0:T(8,128)}, f32[2048,128]{1,0:T(8,128)S(1)}, u32[]{:S(2)}, u32[]{:S(2)}) collective-permute-start(f32[2048,128]{1,0:T(8,128)} %shard_map.58.a), channel_id=1, source_target_pairs={{0,16},{4,20},{24,8},{28,12},{1,17},{5,21},{25,9},{29,13},{2,18},{... | collective-permute-start | bytes 3145736 | tf_op jit(solution)/shard_map/ppermute | solution.py:266
  87.2 23.8 %collective-permute-start.7 = (f32[2048,128]{1,0:T(8,128)}, f32[2048,128]{1,0:T(8,128)S(1)}, u32[]{:S(2)}, u32[]{:S(2)}) collective-permute-start(f32[2048,128]{1,0:T(8,128)} %shard_map.58.a), channel_id=1, source_target_pairs={{8,16},{12,20},{16,8},{20,12},{9,17},{13,21},{17,9},{21,13},{10,18... | collective-permute-start | bytes 3145736 | tf_op jit(solution)/shard_map/ppermute | solution.py:266
  88.0 43.9 %collective-permute-start.13 = (f32[2048,128]{1,0:T(8,128)}, f32[2048,128]{1,0:T(8,128)}, u32[]{:S(2)}, u32[]{:S(2)}) collective-permute-start(f32[2048,128]{1,0:T(8,128)} %shard_map.58.a), channel_id=1, source_target_pairs={{0,8},{4,12},{8,0},{12,4},{16,24},{20,28},{24,16},{28,20},{1,9},{5... | collective-permute-start | bytes 3145736 | tf_op jit(solution)/shard_map/ppermute | solution.py:266
  111.1 20.8 %copy-start.1 = (f32[2048,128]{1,0:T(8,128)}, f32[2048,128]{1,0:T(8,128)S(1)}, u32[]{:S(2)}) copy-start(f32[2048,128]{1,0:T(8,128)S(1)} %collective-permute-done.9.c) | copy-start | bytes 3145732
  111.1 20.8 %collective-permute-start.10 = (f32[2048,128]{1,0:T(8,128)S(1)}, f32[2048,128]{1,0:T(8,128)S(1)}, u32[]{:S(2)}, u32[]{:S(2)}) collective-permute-start(f32[2048,128]{1,0:T(8,128)S(1)} %collective-permute-done.9.c), channel_id=1, source_target_pairs={{0,4},{4,0},{8,12},{12,8},{16,20},{20,16},{24,28},{28,24},{1,5},{5... | collective-permute-start | bytes 3145736 | tf_op jit(solution)/shard_map/ppermute | solution.py:266
  111.1 20.8 %copy-start.2 = (f32[2048,128]{1,0:T(8,128)}, f32[2048,128]{1,0:T(8,128)S(1)}, u32[]{:S(2)}) copy-start(f32[2048,128]{1,0:T(8,128)S(1)} %collective-permute-done.7.a) | copy-start | bytes 3145732
  111.1 20.8 %collective-permute-start.8 = (f32[2048,128]{1,0:T(8,128)S(1)}, f32[2048,128]{1,0:T(8,128)}, u32[]{:S(2)}, u32[]{:S(2)}) collective-permute-start(f32[2048,128]{1,0:T(8,128)S(1)} %collective-permute-done.7.a), channel_id=1, source_target_pairs={{0,4},{4,0},{8,12},{12,8},{16,20},{20,16},{24,28},{28,24},{1,5},{5... | collective-permute-start | bytes 3145736 | tf_op jit(solution)/shard_map/ppermute | solution.py:266
  111.6 29.5 %collective-permute-start.12 = (f32[2048,128]{1,0:T(8,128)}, f32[2048,128]{1,0:T(8,128)}, u32[]{:S(2)}, u32[]{:S(2)}) collective-permute-start(f32[2048,128]{1,0:T(8,128)} %shard_map.58.a), channel_id=1, source_target_pairs={{0,4},{4,0},{8,12},{12,8},{16,20},{20,16},{24,28},{28,24},{1,5},{5... | collective-permute-start | bytes 3145736 | tf_op jit(solution)/shard_map/ppermute | solution.py:266
  131.9 9.3 %collective-permute-start.14 = (f32[2048,128]{1,0:T(8,128)}, f32[2048,128]{1,0:T(8,128)}, u32[]{:S(2)}, u32[]{:S(2)}) collective-permute-start(f32[2048,128]{1,0:T(8,128)} %collective-permute-done.13.c), channel_id=1, source_target_pairs={{0,4},{4,0},{8,12},{12,8},{16,20},{20,16},{24,28},{28,24},{1,5},{5... | collective-permute-start | bytes 3145736 | tf_op jit(solution)/shard_map/ppermute | solution.py:266
  131.9 1.0 copy-start.3
  139.8 28.9 %collective-permute-start.11 = (f32[2048,128]{1,0:T(8,128)}, f32[2048,128]{1,0:T(8,128)S(1)}, u32[]{:S(2)}, u32[]{:S(2)}) collective-permute-start(f32[2048,128]{1,0:T(8,128)} %get-tuple-element.18), channel_id=1, source_target_pairs={{8,0},{12,4},{16,24},{20,28},{9,1},{13,5},{17,25},{21,29},{10,2},{... | collective-permute-start | bytes 3145736 | tf_op jit(solution)/shard_map/ppermute | solution.py:266
  141.1 27.6 %copy-start.9 = (f32[2048,128]{1,0:T(8,128)S(1)}, f32[2048,128]{1,0:T(8,128)}, u32[]{:S(2)}) copy-start(f32[2048,128]{1,0:T(8,128)} %get-tuple-element.17) | copy-start | bytes 3145732
  171.1 27.4 %copy-start = (f32[2048,128]{1,0:T(8,128)}, f32[2048,128]{1,0:T(8,128)S(1)}, u32[]{:S(2)}) copy-start(f32[2048,128]{1,0:T(8,128)S(1)} %get-tuple-element.19.high) | copy-start | bytes 3145732
  171.1 27.4 %collective-permute-start.15 = (f32[2048,128]{1,0:T(8,128)S(1)}, f32[2048,128]{1,0:T(8,128)S(1)}, u32[]{:S(2)}, u32[]{:S(2)}) collective-permute-start(f32[2048,128]{1,0:T(8,128)S(1)} %get-tuple-element.19.high), channel_id=1, source_target_pairs={{0,1},{1,2},{2,3},{4,5},{5,6},{6,7},{8,9},{9,10},{10,11},{12,13},{... | collective-permute-start | bytes 3145736 | tf_op jit(solution)/shard_map/ppermute | solution.py:282
  198.5 1.0 copy-start.7
